TPU v7x, 32 devices: a whole 2x2x4 slice. The times are simulated.
32 devices in a mesh: gx: 8 (over y, x, core), gy: 4 (over z).
Axes of the slice: x: 2, y: 2, z: 4, core: 2. Of those that a mesh axis runs over, the one named last changes fastest.
Arguments:
- node_disp: float32 [2, 256, 1024], P(None, 'gx', 'gy'), may hold values from -0.24 to 0.24
- node_vel: float32 [2, 256, 1024], P(None, 'gx', 'gy'), may hold values from -6 to 6
- node_mass: float32 [256, 1024], P('gx', 'gy'), may hold values from 0.5 to 2
- zone_mass: float32 [256, 1024], P('gx', 'gy'), may hold values from 0.5 to 2
- zone_energy: float32 [256, 1024], P('gx', 'gy'), may hold values from 0.3 to 7.5
- master_block: bfloat16 [32, 4, 1024], P(('gx', 'gy')), may hold values from -3 to 3, as said below
- owner: int32 [1], replicated, may hold values from 0 to 31
- pair_node: int32 [32, 1024], P(('gx', 'gy')), may hold values from 0 to 8191
- pair_segment: int32 [32, 1024], P(('gx', 'gy')), may hold values from 0 to 1022
- pair_side: int32 [32, 1024], P(('gx', 'gy')), may hold values 0 or 1
- pair_count: int32 [32], P(('gx', 'gy')), may hold values from 0 to 1024, as said below
Outputs:
- new_vel: float32 [2, 256, 1024], P(None, 'gx', 'gy')
- new_disp: float32 [2, 256, 1024], P(None, 'gx', 'gy')
- master_impulse: float32 [3, 1024], P(None, ('gx', 'gy'))
Inputs may be any that keep to these rules, and one draw needn't show every extreme that they name: `pair_node`: local node numbers, row-major over a device's 32 x 256 block. `pair_count`: at most 1024; one device has exactly 1024 in every draw; slots at or past a device's count are not pairs. `master_block`: rows 0 and 1 lie within -0.25 to 0.25.
All inputs are finite; a program needn't handle non-finite values. No bound on the sum of `pair_side` on one device may be relied on, other than what follows from the above.
Results may differ from a plain program's by a relative error of at most 0.0015.
Values may be sent and summed in bfloat16 or wider, within the bound.
A program may use at most 128 MiB of HBM per device.

v0:
```python
import jax
import jax.numpy as jnp
from jax import lax
from jax.sharding import PartitionSpec as P

STIFFNESS = 10.0
GAP_SCALE = 0.05


def spread(block, axis, source):
    block = jnp.where(lax.axis_index(axis) == source, block, jnp.zeros_like(block))
    return lax.psum(block, axis)


def with_halo(cells, sides, width):
    for axis, dim in sides:
        count = lax.axis_size(axis)
        ends = count - 1
        head = lax.slice_in_dim(cells, 0, width, axis=dim)
        tail = lax.slice_in_dim(cells, cells.shape[dim] - width, cells.shape[dim], axis=dim)
        cells = jnp.concatenate(
            [
                lax.ppermute(tail, axis, [(i, (i + 1) % count) for i in range(ends)]),
                cells,
                lax.ppermute(head, axis, [((i + 1) % count, i) for i in range(ends)]),
            ],
            axis=dim,
        )
    return cells


def corner_forces(corner_a, corner_b, corner_c, corner_e, zone_load, zone_live):
    first_dx = 1.0 + corner_c[0] - corner_a[0]
    first_dy = 1.0 + corner_c[1] - corner_a[1]
    second_dx = -1.0 + corner_e[0] - corner_b[0]
    second_dy = 1.0 + corner_e[1] - corner_b[1]
    zone_area = 0.5 * (first_dx * second_dy - second_dx * first_dy)
    safe_area = jnp.where(zone_live, zone_area, 1.0)
    half_press = jnp.where(zone_live, 0.2 * zone_load / safe_area, 0.0)
    force_a = jnp.stack([-half_press * second_dy, half_press * second_dx])
    force_b = jnp.stack([half_press * first_dy, -half_press * first_dx])
    return (safe_area, force_a, force_b, -force_a, -force_b)


def contact_terms(slave_disp, seg_start, seg_end, side_flags, live_mask):
    rel_x = slave_disp[0] - seg_start[0] + 0.5
    rel_y = slave_disp[1] - seg_start[1]
    along_x = 1.0 + seg_end[0] - seg_start[0]
    along_y = seg_end[1] - seg_start[1]
    along_sq = along_x * along_x + along_y * along_y
    length = jnp.sqrt(along_sq)
    fraction = (rel_x * along_x + rel_y * along_y) / along_sq
    normal_x = -along_y / length
    normal_y = along_x / length
    gap_size = normal_x * rel_x + normal_y * rel_y
    side_sign = 1.0 - 2.0 * side_flags.astype(jnp.float32)
    magnitude = jnp.where(
        live_mask, STIFFNESS * GAP_SCALE * jax.nn.softplus(-side_sign * gap_size / GAP_SCALE), 0.0
    )
    slave_push = jnp.stack([magnitude * side_sign * normal_x, magnitude * side_sign * normal_y])
    react_first = jnp.stack(
        [
            -(1.0 - fraction) * slave_push[0],
            -(1.0 - fraction) * slave_push[1],
            (1.0 - fraction) * magnitude,
        ]
    )
    react_second = jnp.stack(
        [-fraction * slave_push[0], -fraction * slave_push[1], fraction * magnitude]
    )
    return (slave_push, react_first, react_second)


def shards(
    node_disp,
    node_vel,
    node_mass,
    zone_mass,
    zone_energy,
    master_block,
    owner,
    pair_node,
    pair_segment,
    pair_side,
    pair_count,
):
    row_count = node_disp.shape[1]
    col_count = node_disp.shape[2]
    row_base = lax.axis_index("gx") * row_count
    col_base = lax.axis_index("gy") * col_count
    total_rows = row_count * lax.axis_size("gx")
    total_cols = col_count * lax.axis_size("gy")
    surface = spread(master_block[0], ("gx", "gy"), owner[0])
    packed = jnp.concatenate([node_disp, (zone_energy * zone_mass)[None]], axis=0)
    extended = with_halo(packed.astype(jnp.bfloat16), (("gx", 1), ("gy", 2)), 1).astype(
        packed.dtype
    )
    zone_rows = row_base - 1 + jnp.arange(row_count + 1, dtype=jnp.int32)
    zone_cols = col_base - 1 + jnp.arange(col_count + 1, dtype=jnp.int32)
    zone_live = (
        (zone_rows[:, None] >= 0)
        & (zone_rows[:, None] < total_rows - 1)
        & (zone_cols[None, :] >= 0)
        & (zone_cols[None, :] < total_cols - 1)
    )
    safe_area, force_a, force_b, force_c, force_e = corner_forces(
        extended[:2, : row_count + 1, : col_count + 1],
        extended[:2, 1:, : col_count + 1],
        extended[:2, 1:, 1:],
        extended[:2, : row_count + 1, 1:],
        extended[2, : row_count + 1, : col_count + 1],
        zone_live,
    )
    node_force = (
        force_a[:, 1:, 1:]
        + force_b[:, :row_count, 1:]
        + force_c[:, :row_count, :col_count]
        + force_e[:, 1:, :col_count]
    )
    own_area = safe_area[1:, 1:]
    own_live = zone_live[1:, 1:]
    zone_ratio = jnp.where(own_live, jnp.sqrt(own_area) / jnp.sqrt(0.56 * zone_energy), 1e30)
    step_size = 0.3 * lax.pmin(jnp.min(zone_ratio), ("gx", "gy"))
    coords = surface[0:2].astype(jnp.float32)
    flat_disp = node_disp.reshape(2, row_count * col_count)
    live_count = pair_count[0]
    block_count = (live_count + 127) // 128
    surface_nodes = surface.shape[1]

    def contact_block(block_index, loop_state):
        pushed, reaction = loop_state
        first_pair = block_index * 128
        slave_nodes = lax.dynamic_slice_in_dim(pair_node[0], first_pair, 128)
        segment_ids = lax.dynamic_slice_in_dim(pair_segment[0], first_pair, 128)
        side_flags = lax.dynamic_slice_in_dim(pair_side[0], first_pair, 128)
        live_mask = first_pair + jnp.arange(128, dtype=jnp.int32) < live_count
        slave_disp = jnp.take(flat_disp, slave_nodes, axis=1)
        seg_start = jnp.take(coords, segment_ids, axis=1)
        seg_end = jnp.take(coords, segment_ids + 1, axis=1)
        slave_push, react_first, react_second = contact_terms(
            slave_disp, seg_start, seg_end, side_flags, live_mask
        )
        pushed = pushed.at[:, slave_nodes].add(slave_push)
        reaction = (
            reaction.at[:, segment_ids].add(react_first).at[:, segment_ids + 1].add(react_second)
        )
        return (pushed, reaction)

    pushed, reaction = lax.fori_loop(
        0,
        block_count,
        contact_block,
        (
            jnp.zeros((2, row_count * col_count), jnp.float32),
            jnp.zeros((3, surface_nodes), jnp.float32),
        ),
    )
    total_force = node_force + pushed.reshape(2, row_count, col_count)
    new_vel = node_vel + step_size * total_force / node_mass
    new_disp = node_disp + step_size * new_vel
    share_width = surface_nodes // (lax.axis_size("gx") * lax.axis_size("gy"))
    my_index = lax.axis_index("gx") * lax.axis_size("gy") + lax.axis_index("gy")
    summed = lax.psum(reaction, ("gx", "gy"))
    reaction_share = lax.dynamic_slice_in_dim(summed, my_index * share_width, share_width, 1)
    prior_impulse = lax.dynamic_slice_in_dim(
        surface[2:4], my_index * share_width, share_width, 1
    ).astype(jnp.float32)
    master_impulse = jnp.concatenate(
        [prior_impulse + step_size * reaction_share[0:2], step_size * reaction_share[2:3]], axis=0
    )
    return (new_vel, new_disp, master_impulse)


def solution(mesh):
    in_specs = (
        P(None, "gx", "gy"),
        P(None, "gx", "gy"),
        P("gx", "gy"),
        P("gx", "gy"),
        P("gx", "gy"),
        P(("gx", "gy"), None, None),
        P(),
        P(("gx", "gy"), None),
        P(("gx", "gy"), None),
        P(("gx", "gy"), None),
        P(("gx", "gy")),
    )
    out_specs = (P(None, "gx", "gy"), P(None, "gx", "gy"), P(None, ("gx", "gy")))
    return jax.shard_map(shards, mesh=mesh, in_specs=in_specs, out_specs=out_specs, check_vma=False)
```

profile of v0, /device:TPU:0, one launch (start us, length us, event | category | flops | bytes accessed | tf_op | source)
XLA Modules:
  0.0 288.3 jit_solution(1729171996044898759)
XLA Ops:
  2.3 2.4 collective-permute-start
  6.6 3.4 %copy.43 = f32[2,32,256]{0,2,1:T(8,128)} copy(f32[2,32,256]{2,1,0:T(8,128)} %param.15) | data formatting | bytes 131072 | tf_op args[0]
  10.7 44.0 %psum.14 = bf16[4,1024]{1,0:T(4,128)(2,1)S(1)} all-reduce(bf16[4,1024]{1,0:T(4,128)(2,1)S(1)} %select_bitcast_fusion.3), channel_id=1, replica_groups=mesh['gx'=8,'gy'=4] {'gx','gy'}, use_global_device_ids=true, to_apply=%region_2.3 | all-reduce | flops 4096 | bytes 16384 | tf_op jit(solution)/shard_map/psum | solution.py:12
  54.9 2.2 broadcast_in_dim.60
  57.2 51.2 %while.14 = (s32[]{:T(128)}, f32[2,8192]{0,1:T(8,128)}, f32[3,1024]{0,1:T(8,128)S(1)}, s32[]{:T(128)}, s32[1,1024]{1,0:T(1,128)}, /*index=5*/s32[]{:T(128)}, s32...) while((s32[]{:T(128)}, f32[2,8192]{0,1:T(8,128)}, ...), condition=%wide.region_7.9_spmd, body=%wide.region_3.8_spmd.sunk | while | flops 17542 | bytes 83919 | solution.py:149
  58.6 2.8 gather_fusion.2
  65.8 5.3 %scatter_fusion = f32[2,8192]{0,1:T(8,128)} fusion(f32[2,8192]{0,1:T(8,128)} %get-tuple-element.335, s32[128]{0:T(128)S(1)} %get-tuple-element.302, f32[128,2]{1,0:T(8,128)S(1)} %copy.57), kind=kCustom, calls=%fused_computation.3.clone.1 | custom fusion | flops 256 | bytes 3584 | tf_op jit(solution)/shard_map/while/body/scatter-add | solution.py:143
  71.2 1.5 scatter_fusion.1
  72.8 1.5 scatter_fusion.2
  75.6 2.8 gather_fusion.2
  80.7 1.4 negate_multiply_fusion.9
  82.9 5.3 %scatter_fusion = f32[2,8192]{0,1:T(8,128)} fusion(f32[2,8192]{0,1:T(8,128)} %get-tuple-element.335, s32[128]{0:T(128)S(1)} %get-tuple-element.302, f32[128,2]{1,0:T(8,128)S(1)} %copy.57), kind=kCustom, calls=%fused_computation.3.clone.1 | custom fusion | flops 256 | bytes 3584 | tf_op jit(solution)/shard_map/while/body/scatter-add | solution.py:143
  88.3 1.5 scatter_fusion.1
  89.9 1.5 scatter_fusion.2
  92.7 2.8 gather_fusion.2
  97.8 1.4 negate_multiply_fusion.9
  99.9 5.3 %scatter_fusion = f32[2,8192]{0,1:T(8,128)} fusion(f32[2,8192]{0,1:T(8,128)} %get-tuple-element.335, s32[128]{0:T(128)S(1)} %get-tuple-element.302, f32[128,2]{1,0:T(8,128)S(1)} %copy.57), kind=kCustom, calls=%fused_computation.3.clone.1 | custom fusion | flops 256 | bytes 3584 | tf_op jit(solution)/shard_map/while/body/scatter-add | solution.py:143
  105.4 1.5 scatter_fusion.1
  107.0 1.5 scatter_fusion.2
  108.8 121.9 %psum.15 = f32[3,1024]{1,0:T(4,128)S(1)} all-reduce(f32[3,1024]{1,0:T(4,128)S(1)} %copy.46), channel_id=1, replica_groups=mesh['gx'=8,'gy'=4] {'gx','gy'}, use_global_device_ids=true, to_apply=%region_8.10 | all-reduce | flops 3072 | bytes 24576 | tf_op jit(solution)/shard_map/psum | solution.py:163
  230.8 4.8 %collective-permute-start.2 = (bf16[3,34,1]{2,1,0:T(8,128)(2,1)S(1)}, bf16[3,34,1]{2,1,0:T(8,128)(2,1)S(1)}, u32[]{:S(2)}, u32[]{:S(2)}) collective-permute-start(bf16[3,34,1]{2,1,0:T(8,128)(2,1)S(1)} %get-tuple-element.212), channel_id=1, source_target_pairs={{0,1},{1,2},{2,3},{4,5},{5,6},{6,7},{8,9},{9,10},{10,11},{12,13},{... | collective-permute-start | bytes 620 | tf_op jit(solution)/shard_map/ppermute | solution.py:23
  237.1 4.2 %collective-permute-done.3 = bf16[3,34,1]{2,1,0:T(8,128)(2,1)S(1)} collective-permute-done((bf16[3,34,1]{2,1,0:T(8,128)(2,1)S(1)}, bf16[3,34,1]{2,1,0:T(8,128)(2,1)S(1)}, u32[]{:S(2)}, u32[]{:S(2)}) %collective-permute-start.3) | collective-permute-done | bytes 236 | tf_op jit(solution)/shard_map/ppermute | solution.py:25
  242.4 2.8 copy.47
  245.2 40.9 %pmin.7 = f32[]{:T(128)} all-reduce(f32[]{:T(128)} %fusion.24), channel_id=1, replica_groups=mesh['gx'=8,'gy'=4] {'gx','gy'}, use_global_device_ids=true, to_apply=%region_1.2 | all-reduce | flops 1 | bytes 8 | tf_op jit(solution)/shard_map/pmin | solution.py:123
  (107 shorter events, 22.8 us)
Async XLA Ops:
  0.6 10.0 %copy-start.4 = (bf16[1,4,1024]{2,1,0:T(4,128)(2,1)S(1)}, bf16[1,4,1024]{2,1,0:T(4,128)(2,1)}, u32[]{:S(2)}) copy-start(bf16[1,4,1024]{2,1,0:T(4,128)(2,1)} %param.20) | copy-start | bytes 24580
  2.3 228.4 %collective-permute-start = (bf16[3,1,256]{2,1,0:T(2,128)(2,1)S(1)}, bf16[3,1,256]{2,1,0:T(2,128)(2,1)S(1)}, u32[]{:S(2)}, u32[]{:S(2)}) collective-permute-start(bf16[3,1,256]{2,1,0:T(2,128)(2,1)S(1)} %get-tuple-element.214), channel_id=1, source_target_pairs={{0,4},{4,8},{8,12},{12,16},{16,20},{20,24},{24,28},{1,5},{5,9},{9,... | collective-permute-start | bytes 4616 | tf_op jit(solution)/shard_map/ppermute | solution.py:23
  4.7 226.0 %collective-permute-start.1 = (bf16[3,1,256]{2,1,0:T(2,128)(2,1)S(1)}, bf16[3,1,256]{2,1,0:T(2,128)(2,1)S(1)}, u32[]{:S(2)}, u32[]{:S(2)}) collective-permute-start(bf16[3,1,256]{2,1,0:T(2,128)(2,1)S(1)} %get-tuple-element.215), channel_id=1, source_target_pairs={{4,0},{8,4},{12,8},{16,12},{20,16},{24,20},{28,24},{5,1},{9,5},{13... | collective-permute-start | bytes 4616 | tf_op jit(solution)/shard_map/ppermute | solution.py:25
  54.9 186.7 %copy-start.1 = (f32[32,256]{1,0:T(8,128)S(1)}, f32[32,256]{1,0:T(8,128)}, u32[]{:S(2)}) copy-start(f32[32,256]{1,0:T(8,128)} %param.19) | copy-start | bytes 98308
  108.4 179.1 %copy-start = (f32[2,32,256]{2,1,0:T(8,128)S(1)}, f32[2,32,256]{2,1,0:T(8,128)}, u32[]{:S(2)}) copy-start(f32[2,32,256]{2,1,0:T(8,128)} %param.15) | copy-start | bytes 196612
  108.4 179.1 %copy-start.2 = (f32[2,32,256]{2,1,0:T(8,128)S(1)}, f32[2,32,256]{2,1,0:T(8,128)}, u32[]{:S(2)}) copy-start(f32[2,32,256]{2,1,0:T(8,128)} %param.16) | copy-start | bytes 196612
  108.5 179.1 %copy-start.3 = (f32[32,256]{1,0:T(8,128)S(1)}, f32[32,256]{1,0:T(8,128)}, u32[]{:S(2)}) copy-start(f32[32,256]{1,0:T(8,128)} %param.17) | copy-start | bytes 98308
  230.8 6.3 %collective-permute-start.2 = (bf16[3,34,1]{2,1,0:T(8,128)(2,1)S(1)}, bf16[3,34,1]{2,1,0:T(8,128)(2,1)S(1)}, u32[]{:S(2)}, u32[]{:S(2)}) collective-permute-start(bf16[3,34,1]{2,1,0:T(8,128)(2,1)S(1)} %get-tuple-element.212), channel_id=1, source_target_pairs={{0,1},{1,2},{2,3},{4,5},{5,6},{6,7},{8,9},{9,10},{10,11},{12,13},{... | collective-permute-start | bytes 620 | tf_op jit(solution)/shard_map/ppermute | solution.py:23
  235.6 5.8 %collective-permute-start.3 = (bf16[3,34,1]{2,1,0:T(8,128)(2,1)S(1)}, bf16[3,34,1]{2,1,0:T(8,128)(2,1)S(1)}, u32[]{:S(2)}, u32[]{:S(2)}) collective-permute-start(bf16[3,34,1]{2,1,0:T(8,128)(2,1)S(1)} %get-tuple-element.213), channel_id=1, source_target_pairs={{1,0},{2,1},{3,2},{5,4},{6,5},{7,6},{9,8},{10,9},{11,10},{13,12},{... | collective-permute-start | bytes 620 | tf_op jit(solution)/shard_map/ppermute | solution.py:25
where the time goes:
time: 290 us; the launch traced here: 288 us
  blocking collectives  207 us (71%)
  other arithmetic  41.3 us (14%)
  local copies, waits for them, and re-layouts  23 us (8%)
  starting transfers between devices  9.75 us (3%)
  waiting for transfers between devices  4.41 us (2%)
    psum x1, blocking collectives, shards(): summed = lax.psum(reaction, ('gx', 'gy'))  122 us
    psum x1, blocking collectives, spread(): return lax.psum(block, axis)  44 us
    pmin x1, blocking collectives, shards(): step_size = 0.3 * lax.pmin(jnp.min(zone_ratio), ('gx', 'gy'))  40.9 us
    scatter-add x3, other arithmetic, contact_block(): pushed = pushed.at[:, slave_nodes].add(slave_push)  15.9 us
    scatter-add x6, other arithmetic, contact_block(): reaction.at[:, segment_ids].add(react_first).at[:, segment_ids + 1]  8.71 us
    gather x6, local copies, waits for them, and re-layouts, contact_block(): slave_disp = jnp.take(flat_disp, slave_nodes, axis=1)  8.68 us
    ppermute x2, starting transfers between devices, with_halo(): lax.ppermute(tail, axis, [(i, (i + 1) % count) for i in range(ends)])  7.16 us
  transfers between devices with their start and end apart: 4, of which 2 were waited for; matrix products, arithmetic and copies ran while one was open for 20% of the time, Pallas kernels for 0%

commit v1 on v0

--- a/solution.py
+++ b/solution.py
@@ -160,7 +160,7 @@
     new_disp = node_disp + step_size * new_vel
     share_width = surface_nodes // (lax.axis_size("gx") * lax.axis_size("gy"))
     my_index = lax.axis_index("gx") * lax.axis_size("gy") + lax.axis_index("gy")
-    summed = lax.psum(reaction, ("gx", "gy"))
+    summed = jnp.sum(lax.all_gather(reaction, ("gx", "gy")), axis=0)
     reaction_share = lax.dynamic_slice_in_dim(summed, my_index * share_width, share_width, 1)
     prior_impulse = lax.dynamic_slice_in_dim(
         surface[2:4], my_index * share_width, share_width, 1

time: 290 us -> 316 us (1.090)
  blocking collectives: 207 us -> 233 us
    all_gather x0 -> x1, blocking collectives: none -> 133 us  [shards(): summed = jnp.sum(lax.all_gather(reaction, ('gx', 'gy')), axis=0)]
    psum x1 -> x0, blocking collectives: 122 us -> none  [shards(): summed = lax.psum(reaction, ('gx', 'gy'))]
    pmin x1, blocking collectives: 40.9 us -> 55.9 us  [shards(): step_size = 0.3 * lax.pmin(jnp.min(zone_ratio), ('gx', 'gy'))]
  transfers between devices with their start and end apart: 4 -> 4, of which waited for: 2 -> 2; matrix products, arithmetic and copies ran while one was open for 20% -> 18% of each run, Pallas kernels for 0% -> 0%
where the time goes in v1:
time: 316 us; the launch traced here: 314 us
  blocking collectives  233 us (74%)
  other arithmetic  41.4 us (13%)
  local copies, waits for them, and re-layouts  23 us (7%)
  starting transfers between devices  9.17 us (3%)
  waiting for transfers between devices  4.41 us (1%)
    all_gather x1, blocking collectives, shards(): summed = jnp.sum(lax.all_gather(reaction, ('gx', 'gy')), axis=0)  133 us
    pmin x1, blocking collectives, shards(): step_size = 0.3 * lax.pmin(jnp.min(zone_ratio), ('gx', 'gy'))  55.9 us
    psum x1, blocking collectives, spread(): return lax.psum(block, axis)  44 us
    scatter-add x3, other arithmetic, contact_block(): pushed = pushed.at[:, slave_nodes].add(slave_push)  15.9 us
    scatter-add x6, other arithmetic, contact_block(): reaction.at[:, segment_ids].add(react_first).at[:, segment_ids + 1]  8.71 us
    gather x6, local copies, waits for them, and re-layouts, contact_block(): slave_disp = jnp.take(flat_disp, slave_nodes, axis=1)  8.68 us
    ppermute x2, starting transfers between devices, with_halo(): lax.ppermute(tail, axis, [(i, (i + 1) % count) for i in range(ends)])  6.59 us
  transfers between devices with their start and end apart: 4, of which 2 were waited for; matrix products, arithmetic and copies ran while one was open for 18% of the time, Pallas kernels for 0%

profile of v1, /device:TPU:0, one launch (start us, length us, event | category | flops | bytes accessed | tf_op | source)
XLA Modules:
  0.0 314.3 jit_solution(3295217070302964298)
XLA Ops:
  2.3 2.4 collective-permute-start
  6.6 3.4 %copy.65 = f32[2,32,256]{0,2,1:T(8,128)} copy(f32[2,32,256]{2,1,0:T(8,128)} %param.15) | data formatting | bytes 131072 | tf_op args[0]
  10.7 44.0 %psum.7 = bf16[4,1024]{1,0:T(4,128)(2,1)S(1)} all-reduce(bf16[4,1024]{1,0:T(4,128)(2,1)S(1)} %select_bitcast_fusion.3), channel_id=1, replica_groups=mesh['gx'=8,'gy'=4] {'gx','gy'}, use_global_device_ids=true, to_apply=%region_2.3 | all-reduce | flops 4096 | bytes 16384 | tf_op jit(solution)/shard_map/psum | solution.py:12
  54.9 2.2 broadcast_in_dim.60
  57.2 51.2 %while.14 = (s32[]{:T(128)}, f32[2,8192]{0,1:T(8,128)}, f32[3,1024]{0,1:T(8,128)S(1)}, s32[]{:T(128)}, s32[1,1024]{1,0:T(1,128)}, /*index=5*/s32[]{:T(128)}, s32...) while((s32[]{:T(128)}, f32[2,8192]{0,1:T(8,128)}, ...), condition=%wide.region_7.9_spmd, body=%wide.region_3.8_spmd.sunk | while | flops 17542 | bytes 83919 | solution.py:149
  58.6 2.8 gather_fusion.2
  65.8 5.3 %scatter_fusion = f32[2,8192]{0,1:T(8,128)} fusion(f32[2,8192]{0,1:T(8,128)} %get-tuple-element.348, s32[128]{0:T(128)S(1)} %get-tuple-element.315, f32[128,2]{1,0:T(8,128)S(1)} %copy.88), kind=kCustom, calls=%fused_computation.3.clone.1 | custom fusion | flops 256 | bytes 3584 | tf_op jit(solution)/shard_map/while/body/scatter-add | solution.py:143
  71.2 1.5 scatter_fusion.1
  72.8 1.5 scatter_fusion.2
  75.6 2.8 gather_fusion.2
  80.7 1.4 negate_multiply_fusion.9
  82.9 5.3 %scatter_fusion = f32[2,8192]{0,1:T(8,128)} fusion(f32[2,8192]{0,1:T(8,128)} %get-tuple-element.348, s32[128]{0:T(128)S(1)} %get-tuple-element.315, f32[128,2]{1,0:T(8,128)S(1)} %copy.88), kind=kCustom, calls=%fused_computation.3.clone.1 | custom fusion | flops 256 | bytes 3584 | tf_op jit(solution)/shard_map/while/body/scatter-add | solution.py:143
  88.3 1.5 scatter_fusion.1
  89.9 1.5 scatter_fusion.2
  92.7 2.8 gather_fusion.2
  97.8 1.4 negate_multiply_fusion.9
  99.9 5.3 %scatter_fusion = f32[2,8192]{0,1:T(8,128)} fusion(f32[2,8192]{0,1:T(8,128)} %get-tuple-element.348, s32[128]{0:T(128)S(1)} %get-tuple-element.315, f32[128,2]{1,0:T(8,128)S(1)} %copy.88), kind=kCustom, calls=%fused_computation.3.clone.1 | custom fusion | flops 256 | bytes 3584 | tf_op jit(solution)/shard_map/while/body/scatter-add | solution.py:143
  105.4 1.5 scatter_fusion.1
  106.9 1.5 scatter_fusion.2
  108.8 133.4 %all-gather.1 = f32[32,3,1024]{2,1,0:T(4,128)S(1)} all-gather(f32[1,3,1024]{2,1,0:T(4,128)S(1)} %bitcast.76), channel_id=2, replica_groups=mesh['gx'=8,'gy'=4] {'gx','gy'}, dimensions={0}, use_global_device_ids=true | all-gather | bytes 405504 | tf_op jit(solution)/shard_map/all_gather | solution.py:163
  242.4 4.2 %collective-permute-start.2 = (bf16[3,34,1]{2,1,0:T(8,128)(2,1)S(1)}, bf16[3,34,1]{2,1,0:T(8,128)(2,1)S(1)}, u32[]{:S(2)}, u32[]{:S(2)}) collective-permute-start(bf16[3,34,1]{2,1,0:T(8,128)(2,1)S(1)} %get-tuple-element.225), channel_id=1, source_target_pairs={{0,1},{1,2},{2,3},{4,5},{5,6},{6,7},{8,9},{9,10},{10,11},{12,13},{... | collective-permute-start | bytes 620 | tf_op jit(solution)/shard_map/ppermute | solution.py:23
  248.2 4.2 %collective-permute-done.3 = bf16[3,34,1]{2,1,0:T(8,128)(2,1)S(1)} collective-permute-done((bf16[3,34,1]{2,1,0:T(8,128)(2,1)S(1)}, bf16[3,34,1]{2,1,0:T(8,128)(2,1)S(1)}, u32[]{:S(2)}, u32[]{:S(2)}) %collective-permute-start.3) | collective-permute-done | bytes 236 | tf_op jit(solution)/shard_map/ppermute | solution.py:25
  253.4 2.8 copy.71
  256.2 55.9 %pmin.7 = f32[]{:T(128)} all-reduce(f32[]{:T(128)} %fusion.24), channel_id=1, replica_groups=mesh['gx'=8,'gy'=4] {'gx','gy'}, use_global_device_ids=true, to_apply=%region_1.2 | all-reduce | flops 1 | bytes 8 | tf_op jit(solution)/shard_map/pmin | solution.py:123
  (108 shorter events, 22.9 us)
Async XLA Ops:
  0.6 10.0 %copy-start.4 = (bf16[1,4,1024]{2,1,0:T(4,128)(2,1)S(1)}, bf16[1,4,1024]{2,1,0:T(4,128)(2,1)}, u32[]{:S(2)}) copy-start(bf16[1,4,1024]{2,1,0:T(4,128)(2,1)} %param.20) | copy-start | bytes 24580
  2.3 240.0 %collective-permute-start = (bf16[3,1,256]{2,1,0:T(2,128)(2,1)S(1)}, bf16[3,1,256]{2,1,0:T(2,128)(2,1)S(1)}, u32[]{:S(2)}, u32[]{:S(2)}) collective-permute-start(bf16[3,1,256]{2,1,0:T(2,128)(2,1)S(1)} %get-tuple-element.227), channel_id=1, source_target_pairs={{0,4},{4,8},{8,12},{12,16},{16,20},{20,24},{24,28},{1,5},{5,9},{9,... | collective-permute-start | bytes 4616 | tf_op jit(solution)/shard_map/ppermute | solution.py:23
  4.7 237.6 %collective-permute-start.1 = (bf16[3,1,256]{2,1,0:T(2,128)(2,1)S(1)}, bf16[3,1,256]{2,1,0:T(2,128)(2,1)S(1)}, u32[]{:S(2)}, u32[]{:S(2)}) collective-permute-start(bf16[3,1,256]{2,1,0:T(2,128)(2,1)S(1)} %get-tuple-element.228), channel_id=1, source_target_pairs={{4,0},{8,4},{12,8},{16,12},{20,16},{24,20},{28,24},{5,1},{9,5},{13... | collective-permute-start | bytes 4616 | tf_op jit(solution)/shard_map/ppermute | solution.py:25
  57.2 195.5 %copy-start.1 = (f32[32,256]{1,0:T(8,128)S(1)}, f32[32,256]{1,0:T(8,128)}, u32[]{:S(2)}) copy-start(f32[32,256]{1,0:T(8,128)} %param.19) | copy-start | bytes 98308
  108.4 205.1 %copy-start = (f32[2,32,256]{2,1,0:T(8,128)S(1)}, f32[2,32,256]{2,1,0:T(8,128)}, u32[]{:S(2)}) copy-start(f32[2,32,256]{2,1,0:T(8,128)} %param.15) | copy-start | bytes 196612
  108.4 205.1 %copy-start.2 = (f32[2,32,256]{2,1,0:T(8,128)S(1)}, f32[2,32,256]{2,1,0:T(8,128)}, u32[]{:S(2)}) copy-start(f32[2,32,256]{2,1,0:T(8,128)} %param.16) | copy-start | bytes 196612
  108.4 205.1 %copy-start.3 = (f32[32,256]{1,0:T(8,128)S(1)}, f32[32,256]{1,0:T(8,128)}, u32[]{:S(2)}) copy-start(f32[32,256]{1,0:T(8,128)} %param.17) | copy-start | bytes 98308
  242.4 5.8 %collective-permute-start.2 = (bf16[3,34,1]{2,1,0:T(8,128)(2,1)S(1)}, bf16[3,34,1]{2,1,0:T(8,128)(2,1)S(1)}, u32[]{:S(2)}, u32[]{:S(2)}) collective-permute-start(bf16[3,34,1]{2,1,0:T(8,128)(2,1)S(1)} %get-tuple-element.225), channel_id=1, source_target_pairs={{0,1},{1,2},{2,3},{4,5},{5,6},{6,7},{8,9},{9,10},{10,11},{12,13},{... | collective-permute-start | bytes 620 | tf_op jit(solution)/shard_map/ppermute | solution.py:23
  246.6 5.8 %collective-permute-start.3 = (bf16[3,34,1]{2,1,0:T(8,128)(2,1)S(1)}, bf16[3,34,1]{2,1,0:T(8,128)(2,1)S(1)}, u32[]{:S(2)}, u32[]{:S(2)}) collective-permute-start(bf16[3,34,1]{2,1,0:T(8,128)(2,1)S(1)} %get-tuple-element.226), channel_id=1, source_target_pairs={{1,0},{2,1},{3,2},{5,4},{6,5},{7,6},{9,8},{10,9},{11,10},{13,12},{... | collective-permute-start | bytes 620 | tf_op jit(solution)/shard_map/ppermute | solution.py:25
